TPU v7x, 32 devices: a whole 2x2x4 slice. The times are simulated.
32 devices in a mesh: pool: 2 (over y), blk: 4 (over x, core), batch: 4 (over z).
Axes of the slice: x: 2, y: 2, z: 4, core: 2. Of those that a mesh axis runs over, the one named last changes fastest.
Arguments:
- prompt: bfloat16 [8, 512, 4096], P(('pool', 'batch'), 'blk'), may hold values from -40 to 40
- prompt_len: int32 [2, 4], P('pool', 'batch'), may hold values from 128 to 512
- dec_tokens: bfloat16 [4, 32, 4096], P(None, ('pool', 'batch')), may hold values from -40 to 40
- cache_k: bfloat16 [32, 4096, 1024], P(('pool', 'batch'), None, 'blk'), may hold values from -72 to 72
- cache_v: bfloat16 [32, 4096, 1024], P(('pool', 'batch'), None, 'blk'), may hold values from -6 to 6
- cache_len: int32 [32], P(('pool', 'batch')), may hold values from 1 to 4092
- assign: int32 [2, 4], P('pool', 'batch'), may hold values from 0 to 3, each once within a row
- slot: int32 [2, 4], P('pool', 'batch'), may hold values from 0 to 3
- gain: float32 [4096], replicated, may hold values from 0.5 to 1.5
- w_qkv: bfloat16 [4096, 6144], P(None, 'blk'), may hold values from -4 to 4
- w_out: bfloat16 [4096, 4096], P('blk'), may hold values from -0.09375 to 0.09375
Outputs:
- prefill_out: bfloat16 [8, 512, 4096], P(('pool', 'batch'), 'blk')
- dec_out: bfloat16 [4, 32, 4096], P(None, ('pool', 'batch'))
Inputs may be any that keep to these rules, and one draw needn't show every extreme that they name: For each pool p, assign[p] is a permutation of the 4 stretch indices of the other pool.
All inputs are finite; a program needn't handle non-finite values.
Results may differ from a plain program's by a relative error of at most 0.011.
Values may be sent and summed in bfloat16 or wider, within the bound.
No kernel may reach another device: no remote copies, remote signals or barrier semaphores. Data moves between devices by JAX's collectives and lax.ppermute only.
A program may use at most 128 MiB of HBM per device.

v0:
```python
import jax
import jax.numpy as jnp
from jax import lax
from jax.sharding import PartitionSpec as P

HEAD_DIM = 128
GROUP = 4
EPSILON = 1e-05
THETA = 500000.0


def rms_norm(values, gain):
    wide = values.astype(jnp.float32)
    factor = lax.rsqrt(jnp.mean(wide * wide, axis=-1, keepdims=True) + EPSILON)
    return (wide * factor * gain).astype(jnp.bfloat16)


def rotate(vector, places):
    half = vector.shape[-1] // 2
    freqs = THETA ** (-jnp.arange(half, dtype=jnp.float32) / half)
    angles = places.astype(jnp.float32)[..., None] * freqs
    cosine = jnp.cos(angles)
    sine = jnp.sin(angles)
    first = vector[..., :half]
    second = vector[..., half:]
    return jnp.concatenate(
        [first * cosine - second * sine, second * cosine + first * sine], axis=-1
    )


def softmax_weights(scores):
    top = jnp.max(scores, axis=-1, keepdims=True)
    expo = jnp.exp(scores - top)
    return (expo / jnp.sum(expo, axis=-1, keepdims=True)).astype(jnp.bfloat16)


def make_picker(wanted, carry, piece):
    count = piece[0].shape[0]
    match = jnp.arange(count, dtype=jnp.int32) == wanted
    keys = jnp.sum(jnp.where(match[:, None, None], piece[0].astype(jnp.float32), 0.0), axis=0)
    values = jnp.sum(jnp.where(match[:, None, None], piece[1].astype(jnp.float32), 0.0), axis=0)
    length = carry[2] + jnp.sum(jnp.where(match, piece[2], 0))
    return (keys, values, length)


def attend(
    query,
    cache_key,
    cache_value,
    lengths,
    fresh,
    new_key,
    new_value,
    new_len,
    own_key,
    own_value,
    own_mask,
):
    f32 = jnp.float32
    scale = query.shape[-1] ** (-0.5)
    old = jnp.einsum("srhgd,rchd->srhgc", query, cache_key, preferred_element_type=f32) * scale
    span = jnp.arange(cache_key.shape[1], dtype=jnp.int32)
    old_ok = (span[None, :] < lengths[:, None]) & jnp.logical_not(fresh)[:, None]
    old = jnp.where(old_ok[None, :, None, None, :], old, -jnp.inf)
    new = jnp.einsum("srhgd,chd->srhgc", query, new_key, preferred_element_type=f32) * scale
    reach = jnp.arange(new_key.shape[0], dtype=jnp.int32)
    new_ok = (reach[None, :] < new_len) & fresh[:, None]
    new = jnp.where(new_ok[None, :, None, None, :], new, -jnp.inf)
    own = jnp.einsum("srhgd,trhd->srhgt", query, own_key, preferred_element_type=f32) * scale
    own = jnp.where(own_mask[:, None, None, None, :], own, -jnp.inf)
    cached = cache_key.shape[1]
    fresh_count = new_key.shape[0]
    probs = softmax_weights(jnp.concatenate([old, new, own], axis=-1))
    mixed = jnp.einsum(
        "srhgc,rchd->srhgd", probs[..., :cached], cache_value, preferred_element_type=f32
    )
    mixed = mixed + jnp.einsum(
        "srhgc,chd->srhgd",
        probs[..., cached : cached + fresh_count],
        new_value,
        preferred_element_type=f32,
    )
    mixed = mixed + jnp.einsum(
        "srhgt,trhd->srhgd",
        probs[..., cached + fresh_count :],
        own_value,
        preferred_element_type=f32,
    )
    return mixed.astype(jnp.bfloat16)


def body(
    prompt, prompt_len, dec_tokens, cache_k, cache_v, cache_len, assign, slot, gain, w_qkv, w_out
):
    f32 = jnp.float32
    bf16 = jnp.bfloat16
    local = w_out.shape[0] // (GROUP * HEAD_DIM)
    scale = HEAD_DIM ** (-0.5)
    normed = rms_norm(prompt[0], gain)
    joined = jnp.dot(
        lax.all_gather(normed, "blk", axis=0, tiled=True), w_qkv, preferred_element_type=f32
    )
    stretch = joined.shape[0]
    joined = joined.reshape(stretch, local, GROUP + 2, HEAD_DIM)
    places = jnp.arange(stretch, dtype=jnp.int32)
    query = rotate(joined[:, :, :GROUP], places[:, None, None]).astype(bf16)
    key = rotate(joined[:, :, GROUP], places[:, None]).astype(bf16)
    value = joined[:, :, GROUP + 1].astype(bf16)
    plen = prompt_len[0, 0]
    scores = jnp.einsum("qhgd,khd->hgqk", query, key, preferred_element_type=f32) * scale
    allowed = (places[None, :] <= places[:, None]) & (places[None, :] < plen)
    scores = jnp.where(allowed, scores, -jnp.inf)
    probs = softmax_weights(scores)
    mixed = jnp.einsum("hgqk,khd->qhgd", probs, value, preferred_element_type=f32).astype(bf16)
    mixed = mixed.reshape(stretch, local * GROUP * HEAD_DIM)
    rows = mixed
    summed = lax.psum_scatter(
        jnp.dot(rows, w_out, preferred_element_type=f32).astype(jnp.bfloat16),
        "blk",
        scatter_dimension=0,
        tiled=True,
    ).astype(jnp.float32)
    prefill_out = (prompt[0].astype(f32) + summed).astype(bf16)[None]
    packet = (
        key.reshape(1, stretch, local * HEAD_DIM),
        value.reshape(1, stretch, local * HEAD_DIM),
        prompt_len.reshape(1),
    )
    empty = (
        jnp.zeros((stretch, local * HEAD_DIM), f32),
        jnp.zeros((stretch, local * HEAD_DIM), f32),
        jnp.zeros((), jnp.int32),
    )
    wanted = assign[0, 0]
    source = (1 - lax.axis_index("pool")) * lax.axis_size("batch") + wanted
    arrived = make_picker(
        source,
        empty,
        (
            lax.all_gather(packet[0], ("pool", "batch"), axis=0, tiled=True),
            lax.all_gather(packet[1], ("pool", "batch"), axis=0, tiled=True),
            lax.all_gather(packet[2], ("pool", "batch"), axis=0, tiled=True),
        ),
    )
    new_key = arrived[0].astype(bf16).reshape(stretch, local, HEAD_DIM)
    new_value = arrived[1].astype(bf16).reshape(stretch, local, HEAD_DIM)
    new_len = arrived[2]
    steps = dec_tokens.shape[0]
    rows = dec_tokens.shape[1]
    cached = cache_k.shape[1]
    cache_key = cache_k.reshape(rows, cached, local, HEAD_DIM)
    cache_value = cache_v.reshape(rows, cached, local, HEAD_DIM)
    fresh = jnp.arange(rows, dtype=jnp.int32) == slot[0, 0]
    begin = jnp.where(fresh, new_len, cache_len)
    normed_steps = rms_norm(dec_tokens, gain)
    joined_all = jnp.dot(normed_steps.reshape(steps * rows, -1), w_qkv, preferred_element_type=f32)
    joined_all = joined_all.reshape(steps, rows, local, GROUP + 2, HEAD_DIM)
    where_all = begin[None, :] + jnp.arange(steps, dtype=jnp.int32)[:, None]
    all_query = rotate(joined_all[:, :, :, :GROUP], where_all[:, :, None, None]).astype(bf16)
    all_key = rotate(joined_all[:, :, :, GROUP], where_all[:, :, None]).astype(bf16)
    all_value = joined_all[:, :, :, GROUP + 1].astype(bf16)
    own_mask = jnp.arange(steps)[None, :] <= jnp.arange(steps)[:, None]
    attended = attend(
        all_query,
        cache_key,
        cache_value,
        cache_len,
        fresh,
        new_key,
        new_value,
        new_len,
        all_key,
        all_value,
        own_mask,
    )
    partial_value = jnp.dot(
        attended.reshape(steps * rows, local * GROUP * HEAD_DIM), w_out, preferred_element_type=f32
    )
    total = lax.psum(partial_value.reshape(steps, rows, -1).astype(jnp.bfloat16), "blk").astype(
        jnp.float32
    )
    dec_out = (dec_tokens.astype(f32) + total).astype(bf16)
    return (prefill_out, dec_out)


def solution(mesh):
    return jax.shard_map(
        body,
        mesh=mesh,
        in_specs=(
            P(("pool", "batch"), "blk", None),
            P("pool", "batch"),
            P(None, ("pool", "batch"), None),
            P(("pool", "batch"), None, "blk"),
            P(("pool", "batch"), None, "blk"),
            P(("pool", "batch")),
            P("pool", "batch"),
            P("pool", "batch"),
            P(),
            P(None, "blk"),
            P("blk", None),
        ),
        out_specs=(P(("pool", "batch"), "blk", None), P(None, ("pool", "batch"), None)),
        check_vma=False,
    )
```

profile of v0, /device:TPU:0, one launch (start us, length us, event | category | flops | bytes accessed | tf_op | source)
XLA Modules:
  0.0 270.2 jit_solution(3102997159037806648)
XLA Ops:
  7.2 1.5 fusion.25
  8.8 2.5 fusion.27
  13.3 13.0 %all-reduce = s32[8]{0:T(128)S(1)} all-reduce(s32[8]{0:T(128)S(1)} %bitcast_dynamic-update-slice_fusion), channel_id=2, replica_groups=mesh['pool'=2,'blk'=4,'batch'=4] {'pool','batch'}, use_global_device_ids=true, to_apply=%add | all-reduce | flops 8 | bytes 64 | tf_op jit(solution)/shard_map/all_gather | solution.py:142
  27.6 16.9 %copy.77 = bf16[4096,1536]{0,1:T(8,128)(2,1)} copy(bf16[4096,1536]{1,0:T(8,128)(2,1)} %param.20) | data formatting | bytes 25165824 | tf_op args[9]
  46.1 1.0 multiply_cosine_fusion
  47.1 6.6 %fusion.56 = f32[4,4,2,6,128]{4,1,3,2,0:T(4,128)S(1)} fusion(bf16[2,6,128,4096,1]{3,2,1,0,4:T(8,128)(2,1)} %bitcast.123, bf16[4,4,4096]{2,1,0:T(4,128)(2,1)S(1)} %copy-done.6, f32[4096]{0:T(1024)S(1)} %copy-done.11, f32[4,4]{1,0:T(4,128)S(1)} %add_rsqrt_fusion), kind=kOutput, calls=%fused_computation.73 | convolution fusion | flops 201588736 | bytes 12828736 | tf_op jit(solution)/shard_map/dot_general | solution.py:156
  53.7 10.7 %fusion.79 = f32[512,1536]{0,1:T(8,128)S(1)} fusion(bf16[512,4096]{1,0:T(8,128)(2,1)} %all-gather.5.cloned.1.call-done, bf16[4096,1536]{1,0:T(8,128)(2,1)} %param.20), kind=kOutput, calls=%fused_computation.120 | convolution fusion | flops 6442450944 | bytes 19922944 | tf_op jit(solution)/shard_map/dot_general | solution.py:100
  64.4 1.6 copy-done.1
  72.0 1.1 fusion.47
  73.1 0.9 copy.89
  74.8 12.5 %reshape.382 = bf16[4,4096,2,128]{3,2,1,0:T(2,128)(2,1)} reshape(bf16[4,4096,256]{2,1,0:T(8,128)(2,1)} %param.14) | data formatting | bytes 16777216 | tf_op jit(solution)/shard_map/reshape | solution.py:151
  87.3 12.7 %reshape.383 = bf16[4,4096,2,128]{3,2,1,0:T(2,128)(2,1)} reshape(bf16[4,4096,256]{2,1,0:T(8,128)(2,1)} %param.15) | data formatting | bytes 16777216 | tf_op jit(solution)/shard_map/reshape | solution.py:152
  100.1 6.5 %fusion.76 = (f32[4,4,2,4]{3,0,2,1:T(4,128)}, f32[4,4,2,4,4096]{4,3,0,2,1:T(4,128)S(1)}) fusion(bf16[4,4096,2,128,1]{3,2,1,0,4:T(2,128)(2,1)} %bitcast.125, bf16[4,4,2,4,128]{4,1,3,2,0:T(4,128)(2,1)S(1)} %pad_maximum_fusion, pred[4,4096]{1,0:T(4,128)(4,1)S(1)} %fusion.61), kind=kOutput, calls=%fused_computation.118 | convolution fusion | flops 135790464 | bytes 10535424 | tf_op jit(solution)/shard_map/srhgd,rchd->srhgc/dot_general | solution.py:61
  106.6 1.2 fusion.73
  107.8 3.2 %copy.122 = f32[512,2,4,64]{3,0,2,1:T(8,128)} copy(f32[512,2,4,64]{0,3,2,1:T(8,128)} %get-tuple-element.7) | data formatting | bytes 2097152
  110.9 2.0 copy.123
  112.9 2.8 %subtract_convert_fusion = (bf16[512,2,4,64]{3,0,2,1:T(8,128)(2,1)S(1)}, bf16[512,2,4,64]{3,0,2,1:T(8,128)(2,1)S(1)}) fusion(f32[512,2,4,64]{3,0,2,1:T(8,128)} %copy.123, f32[512,2,4,64]{3,0,2,1:T(8,128)} %copy.122, f32[512,64]{1,0:T(8,128)} %copy-done.3, f32[512,64]{1,0:T(8,128)S(1)} %get-tuple-element.16), kind=kLoop, calls=%fused_computation.33 | loop fusion | flops 2097152 | bytes 3407872 | tf_op jit(solution)/shard_map/convert.6
  115.8 1.3 fusion.42
  117.1 5.5 %fusion.74 = (f32[2,4,512]{2,1,0:T(4,128)S(1)}, f32[2,4,512,512]{2,3,1,0:T(8,128)}) fusion(f32[2,512,512,4]{2,1,3,0:T(8,128)S(1)} %fusion.42, pred[512,512]{0,1:T(8,128)(4,1)S(1)} %copy-done.8), kind=kOutput, calls=%fused_computation.116 | output fusion | flops 12583423 | bytes 17055744 | tf_op jit(solution)/shard_map/sub | solution.py:33
  122.6 5.5 %fusion.29 = bf16[2,128,4,512]{3,1,2,0:T(8,128)(2,1)} fusion(f32[2,4,512,512]{2,3,1,0:T(8,128)} %get-tuple-element.19, f32[2,4,512]{2,1,0:T(4,128)S(1)} %get-tuple-element.18, f32[512,2,6,128]{0,3,2,1:T(8,128)} %bitcast.129), kind=kOutput, calls=%fused_computation.34 | convolution fusion | flops 541589504 | bytes 9715712 | tf_op jit(solution)/shard_map/hgqk,khd->qhgd/dot_general | solution.py:114
  128.1 36.8 %all-gather.9.cloned.1.call-done = bf16[8,512,256]{2,1,0:T(8,128)(2,1)} async-done(((bf16[1,512,256]{2,1,0:T(8,128)(2,1)}), bf16[8,512,256]{2,1,0:T(8,128)(2,1)}) %all-gather.9.cloned.1.call-update) | async-done | bytes 2097168 | tf_op jit(solution)/shard_map/all_gather | solution.py:141
  165.0 3.9 %select_reduce_fusion = (bf16[512,256]{1,0:T(8,128)(2,1)}, bf16[512,256]{1,0:T(8,128)(2,1)S(1)}) fusion(bf16[8,512,256]{2,1,0:T(8,128)(2,1)} %all-gather.9.cloned.1.call-done, pred[8]{0:T(512)(128)(4,1)S(1)} %copy-done.16, bf16[8,512,256]{2,1,0:T(8,128)(2,1)} %all-gather.7.cloned.1.call-done), kind=kLoop, calls=%fused_computation.16 | loop fusion | flops 6029312 | bytes 4718600 | tf_op jit(solution)/shard_map/reduce_sum | solution.py:41
  169.4 1.2 fusion.48
  170.6 1.3 divide_convert_fusion.2
  172.0 1.1 copy.90
  173.1 4.7 %fusion.32 = f32[4,4,2,4,128]{4,3,0,2,1:T(4,128)S(1)} fusion(bf16[4,4096,2,128,1]{3,2,1,0,4:T(2,128)(2,1)} %bitcast.124, bf16[4,4,2,4,4612]{4,3,0,2,1:T(4,128)(2,1)S(1)} %divide_convert_fusion.2), kind=kOutput, calls=%fused_computation.38 | convolution fusion | flops 134217728 | bytes 9502720 | tf_op jit(solution)/shard_map/srhgc,rchd->srhgd/dot_general | solution.py:74
  178.3 5.4 %fusion.11 = bf16[4,4,4096]{2,1,0:T(4,128)(2,1)} fusion(bf16[4,4,1024]{2,1,0:T(4,128)(2,1)S(1)} %dot_general.55, bf16[1024,4096]{1,0:T(8,128)(2,1)} %param.21), kind=kOutput, calls=%fused_computation.13 | convolution fusion | flops 134283264 | bytes 8552448 | tf_op jit(solution)/shard_map/dot_general | solution.py:176
  183.8 9.5 %convolution_convert_fusion = bf16[512,4096]{1,0:T(8,128)(2,1)} fusion(bf16[512,1024]{0,1:T(8,128)(2,1)S(1)} %bitcast.140, bf16[1024,4096]{1,0:T(8,128)(2,1)} %param.21), kind=kOutput, calls=%fused_computation.11 | convolution fusion | flops 4297064448 | bytes 13631488 | tf_op jit(solution)/shard_map/dot_general | solution.py:118
  193.3 20.9 %all-reduce.3.cloned.1.call-done = bf16[4,4,4096]{2,1,0:T(4,128)(2,1)} async-done(((bf16[4,4,4096]{2,1,0:T(4,128)(2,1)}), bf16[4,4,4096]{2,1,0:T(4,128)(2,1)}) %all-reduce.3.cloned.1.call-update) | async-done | bytes 131088 | tf_op jit(solution)/shard_map/psum | solution.py:179
  214.2 1.6 fusion.52
  215.8 45.4 %reduce-scatter.2.cloned.1.call-done = bf16[128,4096]{1,0:T(8,128)(2,1)} async-done(((bf16[512,4096]{1,0:T(8,128)(2,1)}), bf16[128,4096]{1,0:T(8,128)(2,1)}) %reduce-scatter.2.cloned.1.call-update) | async-done | bytes 1048592 | tf_op jit(solution)/shard_map/reduce_scatter | solution.py:117
  261.2 2.4 fusion.40
  (90 shorter events, 10.5 us)
Async XLA Ops:
  7.2 4.8 %copy-start.18 = (u32[32]{0:T(128)S(1)}, u32[32]{0:T(128)}, u32[]{:S(2)}) copy-start(u32[32]{0:T(128)} %constant.44) | copy-start | bytes 388
  7.2 46.5 %all-gather.5.cloned.1.call-start = ((), (), s32[]{:S(2)}) async-start(), calls=%async_computation.1 | async-start | bytes 5242880 | tf_op jit(solution)/shard_map/all_gather | solution.py:101
  11.3 116.8 %all-gather.7.cloned.1.call-start = ((), (), s32[]{:S(2)}) async-start(), calls=%async_computation.3 | async-start | bytes 2359296 | tf_op jit(solution)/shard_map/all_gather | solution.py:140
  27.6 18.3 %copy-start.6 = (bf16[4,4,4096]{2,1,0:T(4,128)(2,1)S(1)}, bf16[4,4,4096]{2,1,0:T(4,128)(2,1)}, u32[]{:S(2)}) copy-start(bf16[4,4,4096]{2,1,0:T(4,128)(2,1)} %param.13) | copy-start | bytes 393220
  27.6 19.4 %copy-start.11 = (f32[4096]{0:T(1024)S(1)}, f32[4096]{0:T(1024)}, u32[]{:S(2)}) copy-start(f32[4096]{0:T(1024)} %param.19) | copy-start | bytes 49156
  47.1 19.2 %copy-start.3 = (f32[512,64]{1,0:T(8,128)}, f32[512,64]{1,0:T(8,128)S(1)}, u32[]{:S(2)}) copy-start(f32[512,64]{1,0:T(8,128)S(1)} %get-tuple-element.17) | copy-start | bytes 393220
  64.4 1.6 copy-start.1
  66.0 1.8 copy-start.15
  66.7 20.6 %copy-start.4 = (bf16[512,2,128]{2,0,1:T(8,128)(2,1)}, bf16[512,2,128]{2,0,1:T(8,128)(2,1)S(1)}, u32[]{:S(2)}) copy-start(bf16[512,2,128]{2,0,1:T(8,128)(2,1)S(1)} %maximum_convert_fusion) | copy-start | bytes 786436
  67.7 97.2 %all-gather.9.cloned.1.call-start = ((), (), s32[]{:S(2)}) async-start(), calls=%async_computation.4 | async-start | bytes 2359296 | tf_op jit(solution)/shard_map/all_gather | solution.py:141
  69.0 31.1 %copy-start.9 = (bf16[4,4,2,4,128]{4,1,3,2,0:T(4,128)(2,1)}, bf16[4,4,2,4,128]{4,1,3,2,0:T(4,128)(2,1)S(1)}, u32[]{:S(2)}) copy-start(bf16[4,4,2,4,128]{4,1,3,2,0:T(4,128)(2,1)S(1)} %pad_maximum_fusion) | copy-start | bytes 98308
  74.0 140.2 %all-reduce.3.cloned.1.call-start = ((), (), s32[]{:S(2)}) async-start(), calls=%async_computation.5 | async-start | bytes 262144 | tf_op jit(solution)/shard_map/psum | solution.py:179
  100.1 6.5 %copy-start.2 = (f32[512,1536]{0,1:T(8,128)S(1)}, f32[512,1536]{0,1:T(8,128)}, u32[]{:S(2)}) copy-start(f32[512,1536]{0,1:T(8,128)} %copy-done.1) | copy-start | bytes 9437188
  112.9 2.9 %copy-start.5 = (bf16[512,2,128]{2,0,1:T(8,128)(2,1)S(1)}, bf16[512,2,128]{2,0,1:T(8,128)(2,1)}, u32[]{:S(2)}) copy-start(bf16[512,2,128]{2,0,1:T(8,128)(2,1)} %copy-done.4) | copy-start | bytes 786436
  115.8 1.4 copy-start.8
  122.6 42.3 %copy-start.16 = (pred[8]{0:T(512)(128)(4,1)S(1)}, pred[8]{0:T(512)(128)(4,1)}, u32[]{:S(2)}) copy-start(pred[8]{0:T(512)(128)(4,1)} %iota_compare_fusion.5) | copy-start | bytes 28
  128.1 40.9 %copy-start.10 = (bf16[4,4,2,4,128]{4,1,3,2,0:T(4,128)(2,1)S(1)}, bf16[4,4,2,4,128]{4,1,3,2,0:T(4,128)(2,1)}, u32[]{:S(2)}) copy-start(bf16[4,4,2,4,128]{4,1,3,2,0:T(4,128)(2,1)} %copy-done.9) | copy-start | bytes 98308
  128.1 40.9 %copy-start.14 = (pred[4,512]{1,0:T(4,128)(4,1)S(1)}, pred[4,512]{1,0:T(4,128)(4,1)}, u32[]{:S(2)}) copy-start(pred[4,512]{1,0:T(4,128)(4,1)} %broadcast_and_fusion) | copy-start | bytes 6148
  128.1 41.3 %copy-start.12 = (f32[4,4,2,4]{3,0,2,1:T(4,128)S(1)}, f32[4,4,2,4]{3,0,2,1:T(4,128)}, u32[]{:S(2)}) copy-start(f32[4,4,2,4]{3,0,2,1:T(4,128)} %get-tuple-element.22) | copy-start | bytes 1540
  128.1 41.3 %copy-start.7 = (f32[4,4,2,4,4]{4,3,0,2,1:T(4,128)S(1)}, f32[4,4,2,4,4]{4,3,0,2,1:T(4,128)}, u32[]{:S(2)}) copy-start(f32[4,4,2,4,4]{4,3,0,2,1:T(4,128)} %get-tuple-element.21) | copy-start | bytes 6148
  173.1 5.0 %copy-start.13 = (bf16[4,4,2,128,1]{3,1,2,0,4:T(4,128)(2,1)S(1)}, bf16[4,4,2,128,1]{3,1,2,0,4:T(4,128)(2,1)}, u32[]{:S(2)}) copy-start(bf16[4,4,2,128,1]{3,1,2,0,4:T(4,128)(2,1)} %fusion.66) | copy-start | bytes 24580
  178.3 5.5 %copy-start.17 = (bf16[2,128,4,512]{3,1,2,0:T(8,128)(2,1)S(1)}, bf16[2,128,4,512]{3,1,2,0:T(8,128)(2,1)}, u32[]{:S(2)}) copy-start(bf16[2,128,4,512]{3,1,2,0:T(8,128)(2,1)} %fusion.29) | copy-start | bytes 3145732
  183.7 77.5 %reduce-scatter.2.cloned.1.call-start = ((), (), s32[]{:S(2)}) async-start(), calls=%async_computation.2 | async-start | bytes 5242880 | tf_op jit(solution)/shard_map/reduce_scatter | solution.py:117
  193.3 67.9 %copy-start = (bf16[1,128,4096]{2,1,0:T(8,128)(2,1)S(1)}, bf16[1,128,4096]{2,1,0:T(8,128)(2,1)}, u32[]{:S(2)}) copy-start(bf16[1,128,4096]{2,1,0:T(8,128)(2,1)} %param.11) | copy-start | bytes 3145732
Sparse Core Ops, SparseCore 0:
  11.4 37.1 all-gather.4
  67.8 47.2 all-gather.6
  117.3 47.6 all-gather.8
  183.8 30.3 all-reduce.2
  216.5 44.5 reduce-scatter.1
where the time goes:
time: 272 us; the launch traced here: 270 us
  waiting for transfers between devices  103 us (38%)
  local copies, waits for them, and re-layouts  56.5 us (21%)
  matrix products  51.7 us (19%)
  other arithmetic  29.2 us (11%)
  between operations  16.2 us (6%)
  blocking collectives  13 us (5%)
    reduce_scatter x1, waiting for transfers between devices, body(): lax.psum_scatter(jnp.dot(rows, w_out, preferred_element_type=f32).astype(...  45.4 us
    all_gather x1, waiting for transfers between devices, body(): lax.all_gather(packet[1], ('pool', 'batch'), axis=0, tiled=True)  36.8 us
    unnamed x45, local copies, waits for them, and re-layouts  25.2 us
    psum x1, waiting for transfers between devices, body(): lax.psum(partial_value.reshape(steps, rows, -1).astype(jnp.bfloat16), 'blk')  20.9 us
    all_gather x1, blocking collectives, body(): lax.all_gather(packet[2], ('pool', 'batch'), axis=0, tiled=True)  13 us
    reshape x1, local copies, waits for them, and re-layouts, body(): cache_value = cache_v.reshape(rows, cached, local, HEAD_DIM)  12.7 us
    reshape x1, local copies, waits for them, and re-layouts, body(): cache_key = cache_k.reshape(rows, cached, local, HEAD_DIM)  12.5 us
    dot_general x1, matrix products, body(): jnp.dot(lax.all_gather(normed, 'blk', axis=0, tiled=True), w_qkv, preferr...  10.7 us
  transfers between devices with their start and end apart: 5, of which 3 were waited for; matrix products, arithmetic and copies ran while one was open for 36% of the time, Pallas kernels for 0%

commit v1 on v0

--- a/solution.py
+++ b/solution.py
@@ -176,7 +176,11 @@
     partial_value = jnp.dot(
         attended.reshape(steps * rows, local * GROUP * HEAD_DIM), w_out, preferred_element_type=f32
     )
-    total = lax.psum(partial_value.reshape(steps, rows, -1).astype(jnp.bfloat16), "blk").astype(
+
+    def recast_scales_on(mat):
+        return jnp.sum(jax.lax.all_gather(mat, axis_name="blk"), axis=0)
+
+    total = recast_scales_on(partial_value.reshape(steps, rows, -1).astype(jnp.bfloat16)).astype(
         jnp.float32
     )
     dec_out = (dec_tokens.astype(f32) + total).astype(bf16)

time: 272 us -> 220 us (0.81)
  waiting for transfers between devices: 103 us -> 51 us
  blocking collectives: 13 us -> 21.7 us
  matrix products: 51.7 us -> 46.7 us
    all_gather x1, waiting for transfers between devices: 36.8 us -> 0.02 us  [body(): lax.all_gather(packet[1], ('pool', 'batch'), axis=0, tiled=True)]
    all_gather x1, waiting for transfers between devices: 0.02 us -> 34.2 us  [body(): lax.all_gather(normed, 'blk', axis=0, tiled=True)]
    reduce_scatter x1, waiting for transfers between devices: 45.4 us -> 16.7 us  [body(): lax.psum_scatter(jnp.dot(rows, w_out, preferred_element_type=f32).astype(...]
    psum x1 -> x0, waiting for transfers between devices: 20.9 us -> none  [body(): lax.psum(partial_value.reshape(steps, rows, -1).astype(jnp.bfloat16), 'blk')]
    all_gather x0 -> x1, blocking collectives: none -> 10.4 us  [recast_scales_on(): return jnp.sum(jax.lax.all_gather(mat, axis_name='blk'), axis=0)]
    dot_general x1, matrix products: 9.5 us -> 6.27 us  [body(): jnp.dot(rows, w_out, preferred_element_type=f32).astype(jnp.bfloat16)]
    unnamed x45 -> x41, local copies, waits for them, and re-layouts: 25.2 us -> 24.2 us
  transfers between devices with their start and end apart: 5 -> 4, of which waited for: 3 -> 2; matrix products, arithmetic and copies ran while one was open for 36% -> 50% of each run, Pallas kernels for 0% -> 0%
where the time goes in v1:
time: 220 us; the launch traced here: 219 us
  local copies, waits for them, and re-layouts  55.4 us (25%)
  waiting for transfers between devices  51 us (23%)
  matrix products  46.7 us (21%)
  other arithmetic  27.7 us (13%)
  blocking collectives  21.7 us (10%)
  between operations  16.1 us (7%)
    all_gather x1, waiting for transfers between devices, body(): lax.all_gather(normed, 'blk', axis=0, tiled=True)  34.2 us
    unnamed x41, local copies, waits for them, and re-layouts  24.2 us
    reduce_scatter x1, waiting for transfers between devices, body(): lax.psum_scatter(jnp.dot(rows, w_out, preferred_element_type=f32).astype(...  16.7 us
    reshape x1, local copies, waits for them, and re-layouts, body(): cache_key = cache_k.reshape(rows, cached, local, HEAD_DIM)  12.6 us
    reshape x1, local copies, waits for them, and re-layouts, body(): cache_value = cache_v.reshape(rows, cached, local, HEAD_DIM)  12.6 us
    all_gather x1, blocking collectives, body(): lax.all_gather(packet[2], ('pool', 'batch'), axis=0, tiled=True)  11.3 us
    dot_general x1, matrix products, body(): jnp.dot(lax.all_gather(normed, 'blk', axis=0, tiled=True), w_qkv, preferr...  10.6 us
    all_gather x1, blocking collectives, recast_scales_on(): return jnp.sum(jax.lax.all_gather(mat, axis_name='blk'), axis=0)  10.4 us
  transfers between devices with their start and end apart: 4, of which 2 were waited for; matrix products, arithmetic and copies ran while one was open for 50% of the time, Pallas kernels for 0%

profile of v1, /device:TPU:0, one launch (start us, length us, event | category | flops | bytes accessed | tf_op | source)
XLA Modules:
  0.0 219.0 jit_solution(1300038439614414521)
XLA Ops:
  7.2 1.5 fusion.25
  8.8 2.5 %fusion.27 = bf16[128,4096]{1,0:T(8,128)(2,1)} fusion(bf16[1,128,4096]{2,1,0:T(8,128)(2,1)} %param.11, f32[4096]{0:T(1024)} %param.19, f32[128]{0:T(128)S(1)} %add_rsqrt_fusion.1), kind=kLoop, calls=%fused_computation.30 | loop fusion | flops 2097152 | bytes 2114048 | tf_op jit(solution)/shard_map/convert_element_type | solution.py:15
  13.4 1.0 multiply_cosine_fusion
  14.4 34.2 %all-gather.6.cloned.1.call-done = bf16[512,4096]{1,0:T(8,128)(2,1)} async-done(((bf16[128,4096]{1,0:T(8,128)(2,1)}), bf16[512,4096]{1,0:T(8,128)(2,1)}) %all-gather.6.cloned.1.call-update) | async-done | bytes 4194320 | tf_op jit(solution)/shard_map/all_gather | solution.py:101
  48.6 10.6 %fusion.79 = f32[512,1536]{0,1:T(8,128)S(1)} fusion(bf16[512,4096]{1,0:T(8,128)(2,1)} %all-gather.6.cloned.1.call-done, bf16[4096,1536]{1,0:T(8,128)(2,1)} %param.20), kind=kOutput, calls=%fused_computation.120 | convolution fusion | flops 6442450944 | bytes 19922944 | tf_op jit(solution)/shard_map/dot_general | solution.py:100
  59.3 1.7 copy-done.1
  63.3 11.3 %all-reduce = s32[8]{0:T(128)S(1)} all-reduce(s32[8]{0:T(128)S(1)} %bitcast_dynamic-update-slice_fusion), channel_id=2, replica_groups=mesh['pool'=2,'blk'=4,'batch'=4] {'pool','batch'}, use_global_device_ids=true, to_apply=%add | all-reduce | flops 8 | bytes 64 | tf_op jit(solution)/shard_map/all_gather | solution.py:142
  74.6 16.9 %copy.77 = bf16[4096,1536]{0,1:T(8,128)(2,1)} copy(bf16[4096,1536]{1,0:T(8,128)(2,1)} %param.20) | data formatting | bytes 25165824 | tf_op args[9]
  93.9 1.2 iota_compare_fusion.3
  96.2 0.9 fusion.46
  97.0 7.1 %fusion.56 = f32[4,4,2,6,128]{4,1,3,2,0:T(4,128)} fusion(bf16[2,6,128,4096,1]{3,2,1,0,4:T(8,128)(2,1)} %bitcast.124, bf16[4,4,4096]{2,1,0:T(4,128)(2,1)S(1)} %copy-done.5, f32[4096]{0:T(1024)S(1)} %copy-done.8, f32[4,4]{1,0:T(4,128)S(1)} %add_rsqrt_fusion), kind=kOutput, calls=%fused_computation.73 | convolution fusion | flops 201588736 | bytes 12828736 | tf_op jit(solution)/shard_map/dot_general | solution.py:156
  104.2 1.1 fusion.47
  105.2 0.8 copy.89
  106.1 2.8 %fusion.73 = (f32[512,2,4,64]{0,3,2,1:T(8,128)S(1)}, f32[512,2,4,64]{0,3,2,1:T(8,128)}) fusion(f32[512,2,6,128]{0,3,2,1:T(8,128)} %bitcast.132), kind=kLoop, calls=%fused_computation.115 | loop fusion | bytes 4194304 | tf_op jit(solution)/shard_map/slice | solution.py:25
  108.8 1.8 copy.122
  110.7 1.9 copy.123
  112.8 2.1 subtract_convert_fusion
  115.0 1.4 fusion.42
  116.4 5.6 %fusion.74 = (f32[2,4,512]{2,1,0:T(4,128)S(1)}, f32[2,4,512,512]{2,3,1,0:T(8,128)}) fusion(f32[2,512,512,4]{2,1,3,0:T(8,128)S(1)} %fusion.42, pred[512,512]{0,1:T(8,128)(4,1)S(1)} %copy-done.6), kind=kOutput, calls=%fused_computation.116 | output fusion | flops 12583423 | bytes 17055744 | tf_op jit(solution)/shard_map/sub | solution.py:33
  122.0 4.4 %fusion.29 = bf16[2,128,4,512]{3,1,2,0:T(8,128)(2,1)S(1)} fusion(f32[2,4,512,512]{2,3,1,0:T(8,128)} %get-tuple-element.19, f32[2,4,512]{2,1,0:T(4,128)S(1)} %get-tuple-element.18, f32[512,2,6,128]{0,3,2,1:T(8,128)} %bitcast.133), kind=kOutput, calls=%fused_computation.34 | convolution fusion | flops 541589504 | bytes 9715712 | tf_op jit(solution)/shard_map/hgqk,khd->qhgd/dot_general | solution.py:114
  126.7 6.3 %convolution_convert_fusion = bf16[512,4096]{1,0:T(8,128)(2,1)} fusion(bf16[512,1024]{0,1:T(8,128)(2,1)S(1)} %bitcast.144, bf16[1024,4096]{1,0:T(8,128)(2,1)S(1)} %bitcast.126), kind=kOutput, calls=%fused_computation.11 | convolution fusion | flops 4297064448 | bytes 13631488 | tf_op jit(solution)/shard_map/dot_general | solution.py:118
  133.0 12.6 %reshape.382 = bf16[4,4096,2,128]{3,2,1,0:T(2,128)(2,1)} reshape(bf16[4,4096,256]{2,1,0:T(8,128)(2,1)} %param.14) | data formatting | bytes 16777216 | tf_op jit(solution)/shard_map/reshape | solution.py:151
  145.6 12.6 %reshape.383 = bf16[4,4096,2,128]{3,2,1,0:T(2,128)(2,1)} reshape(bf16[4,4096,256]{2,1,0:T(8,128)(2,1)} %param.15) | data formatting | bytes 16777216 | tf_op jit(solution)/shard_map/reshape | solution.py:152
  159.1 5.8 %fusion.76 = (f32[4,4,2,4]{3,0,2,1:T(4,128)S(1)}, f32[4,4,2,4,4096]{4,3,0,2,1:T(4,128)S(1)}) fusion(bf16[4,4096,2,128,1]{3,2,1,0,4:T(2,128)(2,1)} %bitcast.128, bf16[4,4,2,4,128]{4,1,3,2,0:T(4,128)(2,1)S(1)} %pad_maximum_fusion, pred[4,4096]{1,0:T(4,128)(4,1)S(1)} %fusion.61), kind=kOutput, calls=%fused_computation.118 | convolution fusion | flops 135790464 | bytes 10535424 | tf_op jit(solution)/shard_map/srhgd,rchd->srhgc/dot_general | solution.py:61
  164.9 3.1 %select_reduce_fusion = (bf16[512,256]{1,0:T(8,128)(2,1)S(1)}, bf16[512,256]{1,0:T(8,128)(2,1)S(1)}) fusion(bf16[8,512,256]{2,1,0:T(8,128)(2,1)} %all-gather.10.cloned.1.call-done, pred[8]{0:T(512)(128)(4,1)S(1)} %copy-done.11, bf16[8,512,256]{2,1,0:T(8,128)(2,1)} %all-gather.8.cloned.1.call-done), kind=kLoop, calls=%fused_computation.16 | loop fusion | flops 6029312 | bytes 4718600 | tf_op jit(solution)/shard_map/reduce_sum | solution.py:41
  168.7 1.2 fusion.48
  169.9 1.3 divide_convert_fusion.2
  171.2 5.5 %fusion.32 = f32[4,4,2,4,128]{4,3,0,2,1:T(4,128)S(1)} fusion(bf16[4,4096,2,128,1]{3,2,1,0,4:T(2,128)(2,1)} %bitcast.127, bf16[4,4,2,4,4612]{4,3,0,2,1:T(4,128)(2,1)S(1)} %divide_convert_fusion.2), kind=kOutput, calls=%fused_computation.38 | convolution fusion | flops 134217728 | bytes 9502720 | tf_op jit(solution)/shard_map/srhgc,rchd->srhgd/dot_general | solution.py:74
  177.2 4.7 %fusion.11 = bf16[4,4,4096]{2,1,0:T(4,128)(2,1)S(1)} fusion(bf16[4,4,1024]{2,1,0:T(4,128)(2,1)S(1)} %dot_general.55, bf16[1024,4096]{1,0:T(8,128)(2,1)} %param.21), kind=kOutput, calls=%fused_computation.13 | convolution fusion | flops 134283264 | bytes 8552448 | tf_op jit(solution)/shard_map/dot_general | solution.py:176
  181.9 10.4 %all-gather.1 = bf16[16,4,4096]{2,1,0:T(4,128)(2,1)S(1)} all-gather(bf16[4,4,4096]{2,1,0:T(4,128)(2,1)S(1)} %fusion.11), channel_id=3, replica_groups=mesh['pool'=2,'blk'=4,'batch'=4] {'blk'}, dimensions={0}, use_global_device_ids=true | all-gather | bytes 655360 | tf_op jit(solution)/shard_map/all_gather | solution.py:181
  193.3 16.7 %reduce-scatter.2.cloned.1.call-done = bf16[128,4096]{1,0:T(8,128)(2,1)} async-done(((bf16[512,4096]{1,0:T(8,128)(2,1)}), bf16[128,4096]{1,0:T(8,128)(2,1)}) %reduce-scatter.2.cloned.1.call-update) | async-done | bytes 1048592 | tf_op jit(solution)/shard_map/reduce_scatter | solution.py:117
  210.0 2.4 %fusion.40 = bf16[1,128,4096]{2,1,0:T(8,128)(2,1)} fusion(bf16[128,4096]{1,0:T(8,128)(2,1)} %reduce-scatter.2.cloned.1.call-done, bf16[1,128,4096]{2,1,0:T(8,128)(2,1)S(1)} %copy-done), kind=kLoop, calls=%fused_computation.47 | loop fusion | flops 2097152 | bytes 3145728 | tf_op jit(solution)/shard_map/broadcast_in_dim | solution.py:123
  (86 shorter events, 9.4 us)
Async XLA Ops:
  7.2 4.8 %copy-start.13 = (u32[32]{0:T(128)S(1)}, u32[32]{0:T(128)}, u32[]{:S(2)}) copy-start(u32[32]{0:T(128)} %constant.46) | copy-start | bytes 388
  7.2 41.5 %all-gather.6.cloned.1.call-start = ((), (), s32[]{:S(2)}) async-start(), calls=%async_computation.1 | async-start | bytes 5242880 | tf_op jit(solution)/shard_map/all_gather | solution.py:101
  11.3 153.6 %all-gather.8.cloned.1.call-start = ((), (), s32[]{:S(2)}) async-start(), calls=%async_computation.3 | async-start | bytes 2359296 | tf_op jit(solution)/shard_map/all_gather | solution.py:140
  14.4 46.8 %copy-start.2 = (f32[512,64]{1,0:T(8,128)}, f32[512,64]{1,0:T(8,128)S(1)}, u32[]{:S(2)}) copy-start(f32[512,64]{1,0:T(8,128)S(1)} %get-tuple-element.17) | copy-start | bytes 393220
  59.3 1.7 copy-start.1
  61.6 29.9 %copy-start.3 = (bf16[512,2,128]{2,0,1:T(8,128)(2,1)}, bf16[512,2,128]{2,0,1:T(8,128)(2,1)S(1)}, u32[]{:S(2)}) copy-start(bf16[512,2,128]{2,0,1:T(8,128)(2,1)S(1)} %maximum_convert_fusion) | copy-start | bytes 786436
  62.6 102.3 %all-gather.10.cloned.1.call-start = ((), (), s32[]{:S(2)}) async-start(), calls=%async_computation.4 | async-start | bytes 2359296 | tf_op jit(solution)/shard_map/all_gather | solution.py:141
  74.6 20.6 %copy-start.5 = (bf16[4,4,4096]{2,1,0:T(4,128)(2,1)S(1)}, bf16[4,4,4096]{2,1,0:T(4,128)(2,1)}, u32[]{:S(2)}) copy-start(bf16[4,4,4096]{2,1,0:T(4,128)(2,1)} %param.13) | copy-start | bytes 393220
  74.6 20.7 %copy-start.9 = (s32[4]{0:T(128)S(1)}, s32[4]{0:T(128)}, u32[]{:S(2)}) copy-start(s32[4]{0:T(128)} %param.16) | copy-start | bytes 52
  74.6 22.4 %copy-start.8 = (f32[4096]{0:T(1024)S(1)}, f32[4096]{0:T(1024)}, u32[]{:S(2)}) copy-start(f32[4096]{0:T(1024)} %param.19) | copy-start | bytes 49156
  112.6 2.4 %copy-start.4 = (bf16[512,2,128]{2,0,1:T(8,128)(2,1)S(1)}, bf16[512,2,128]{2,0,1:T(8,128)(2,1)}, u32[]{:S(2)}) copy-start(bf16[512,2,128]{2,0,1:T(8,128)(2,1)} %copy-done.3) | copy-start | bytes 786436
  112.6 97.4 %reduce-scatter.2.cloned.1.call-start = ((), (), s32[]{:S(2)}) async-start(), calls=%async_computation.2 | async-start | bytes 5242880 | tf_op jit(solution)/shard_map/reduce_scatter | solution.py:117
  115.0 1.4 copy-start.6
  116.4 10.0 %slice-start = ((s8[8388608]{0:T(1024)(128)(4,1)}), s8[4194304]{0:T(1024)(128)(4,1)S(1)}, s32[]{:S(2)}) async-start(s8[8388608]{0:T(1024)(128)(4,1)} %bitcast.125), calls=%async_computation.5 | async-start | bytes 8388608
  122.0 4.7 %slice-start.1 = ((s8[8388608]{0:T(1024)(128)(4,1)}), s8[4194304]{0:T(1024)(128)(4,1)S(1)}, s32[]{:S(2)}) async-start(s8[8388608]{0:T(1024)(128)(4,1)} %bitcast.125), calls=%async_computation.6 | async-start | bytes 8388608
  145.6 12.6 %copy-start.7 = (f32[4,4,2,6,128]{4,1,3,2,0:T(4,128)S(1)}, f32[4,4,2,6,128]{4,1,3,2,0:T(4,128)}, u32[]{:S(2)}) copy-start(f32[4,4,2,6,128]{4,1,3,2,0:T(4,128)} %fusion.56) | copy-start | bytes 294916
  145.6 13.0 %copy-start.12 = (pred[512]{0:T(512)(128)(4,1)S(1)}, pred[512]{0:T(512)(128)(4,1)}, u32[]{:S(2)}) copy-start(pred[512]{0:T(512)(128)(4,1)} %iota_compare_fusion.3) | copy-start | bytes 1540
  145.6 13.1 %copy-start.14 = (pred[4,4]{1,0:T(4,128)(4,1)S(1)}, pred[4,4]{1,0:T(4,128)(4,1)}, u32[]{:S(2)}) copy-start(pred[4,4]{1,0:T(4,128)(4,1)} %iota_compare_fusion.2) | copy-start | bytes 52
  145.6 13.3 %copy-start.10 = (s32[4]{0:T(128)S(1)}, s32[4]{0:T(128)}, u32[]{:S(2)}) copy-start(s32[4]{0:T(128)} %param.16) | copy-start | bytes 52
  159.1 5.8 %copy-start.11 = (pred[8]{0:T(512)(128)(4,1)S(1)}, pred[8]{0:T(512)(128)(4,1)}, u32[]{:S(2)}) copy-start(pred[8]{0:T(512)(128)(4,1)} %iota_compare_fusion.5) | copy-start | bytes 28
  177.1 32.8 %copy-start = (bf16[1,128,4096]{2,1,0:T(8,128)(2,1)S(1)}, bf16[1,128,4096]{2,1,0:T(8,128)(2,1)}, u32[]{:S(2)}) copy-start(bf16[1,128,4096]{2,1,0:T(8,128)(2,1)} %param.11) | copy-start | bytes 3145732
Sparse Core Ops, SparseCore 0:
  11.4 37.1 all-gather.5
  62.8 49.0 all-gather.7
  114.0 47.6 all-gather.9
  164.0 45.9 reduce-scatter.1
